TPU v7x, 256 devices: a whole 4x4x8 slice. The times are simulated.
256 devices in a mesh: vert: 16 (over x, y), feat: 16 (over z, core).
Axes of the slice: x: 4, y: 4, z: 8, core: 2. Of those that a mesh axis runs over, the one named last changes fastest.
Arguments:
- features: bfloat16 [131072, 256], P('vert', 'feat'), may hold values from -6 to 6
- tiles: bfloat16 [1024, 16, 128, 128], P('vert'), may hold values from -0.1875 to 0.1875
- tile_cols: int32 [1024, 16], P('vert'), may hold values from 0 to 127
- tile_count: int32 [1024], P('vert'), may hold values from 1 to 16, as said below
- send_list: int32 [16, 16, 4], P('vert'), may hold values from 0 to 63
- weight: bfloat16 [256, 256], replicated, may hold values from -0.375 to 0.375
- bias: float32 [256], replicated, may hold values from -3 to 3
Outputs:
- node_out: bfloat16 [131072, 256], P(('vert', 'feat'))
Inputs may be any that keep to these rules, and one draw needn't show every extreme that they name: Row block r uses tile places 0 to tile_count[r] - 1; in every draw some row block uses all 16.
All inputs are finite; a program needn't handle non-finite values.
Results may differ from a plain program's by a relative error of at most 0.0044.
Values may be sent and summed in bfloat16 or wider, within the bound.
No kernel may reach another device: no remote copies, remote signals or barrier semaphores. Data moves between devices by JAX's collectives and lax.ppermute only.
A program may use at most 128 MiB of HBM per device.

v0:
```python
import jax
import jax.numpy as jnp
from jax import lax
from jax.experimental import pallas as pl
from jax.experimental.pallas import tpu as pltpu
from jax.sharding import PartitionSpec as P

VMEM = pltpu.VMEM
SMEM = pltpu.SMEM
EACH = 24
PAIRS_MAX = 8
ROWS = 64
HALF = ROWS // 2
EDGE = 128
SLOTS = 2 * ROWS + 1
LIST_ROWS = 8
LIST_BLOCKS = 3
LIST_SPAN = LIST_BLOCKS * 128
LENGTH_ROW = 2 * LIST_BLOCKS


def build_list(cols_ref, count_ref, piece_ref, table_ref):
    f32, i32, bf16 = jnp.float32, jnp.int32, jnp.bfloat16
    counts = count_ref[...]
    lane_row = lax.broadcasted_iota(i32, (1, ROWS), 1)
    for p in range(PAIRS_MAX):
        for half in range(2):
            k = 2 * p + half
            slot = jnp.where(counts > k, cols_ref[k:k + 1, :] + 1, 0)
            piece_ref[8 * half + p:8 * half + p + 1, :] = slot.astype(f32)
    piece_ref[16:17, :] = lane_row.astype(f32)
    piece_ref[17:24, :] = jnp.zeros((7, ROWS), f32)
    pairs_each = ((counts + 1) >> 1).astype(f32)
    odd = lane_row & 1
    for part in range(2):
        piece_ref[24 + part:25 + part, :] = jnp.where(odd == part, pairs_each, f32(0))
    piece_ref[26:32, :] = jnp.zeros((6, ROWS), f32)

    pairs = piece_ref[24:32, :].astype(bf16)
    r_out = lax.broadcasted_iota(i32, (2 * ROWS, ROWS), 0)
    r_in = lax.broadcasted_iota(i32, (2 * ROWS, ROWS), 1)
    before = jnp.where(r_out < ROWS, (r_in < r_out).astype(f32), (r_in == r_out - ROWS).astype(f32))
    nt = (((1,), (1,)), ((), ()))
    nn = (((1,), (0,)), ((), ()))
    column = lax.dot_general(before.astype(bf16), pairs, nt, preferred_element_type=f32)
    spot = lax.broadcasted_iota(i32, (ROWS, LIST_SPAN), 1).astype(f32)
    spot_row = lax.broadcasted_iota(i32, (1, LIST_SPAN), 1)
    p_row = lax.broadcasted_iota(i32, (PAIRS_MAX, LIST_SPAN), 0)
    pieces = piece_ref[0:24, :].astype(bf16)
    for part in range(2):
        begin = column[0:ROWS, part:part + 1]
        end = begin + column[ROWS:2 * ROWS, part:part + 1]
        past = spot >= end
        inside = jnp.where((spot >= begin) & jnp.logical_not(past), f32(1), f32(0)).astype(bf16)
        past = jnp.where(past, f32(1), f32(0)).astype(bf16)
        chosen = lax.dot_general(pieces, inside, nn, preferred_element_type=f32)
        ahead = lax.dot_general(pairs, past, nn, preferred_element_type=f32)
        ahead = ahead[part:part + 1, :].astype(i32)
        pair = spot_row - ahead
        mine = p_row == pair

        def field(at):
            return jnp.sum(
                jnp.where(mine, chosen[at:at + PAIRS_MAX, :], f32(0)), axis=0, keepdims=True
            ).astype(i32)

        item = (chosen[16:17, :].astype(i32) << 3) | (field(0) << 9) | (field(8) << 17)
        total = ahead[:, LIST_SPAN - 1:LIST_SPAN]
        item = jnp.where(spot_row < total, item | pair, 0)
        for block in range(LIST_BLOCKS):
            at = part * LIST_BLOCKS + block
            table_ref[at:at + 1, :] = item[:, block * 128:(block + 1) * 128]
        at = LENGTH_ROW + part
        table_ref[at:at + 1, :] = ahead[:, LIST_SPAN - 128:LIST_SPAN]


def pick_kernel(
    send_hbm, feat_hbm, cols_hbm, count_hbm, out_ref, slab_ref, table_ref,
    send_ref, feat_ref, cols_ref, count_ref, piece_ref, sem,
):
    copies = [
        pltpu.make_async_copy(src, dst, sem.at[i])
        for i, (src, dst) in enumerate(
            [(feat_hbm, feat_ref), (cols_hbm, cols_ref), (count_hbm, count_ref), (send_hbm, send_ref)]
        )
    ]
    for copy in copies:
        copy.start()
    copies[1].wait()
    copies[2].wait()
    build_list(cols_ref, count_ref, piece_ref, table_ref)
    copies[3].wait()
    copies[0].wait()
    slots, peers = send_ref.shape
    for peer in range(peers):
        for slot in range(slots):
            start = pl.multiple_of(send_ref[slot, peer] * EDGE, EDGE)
            out_ref[peer * slots + slot] = feat_ref[:, pl.ds(start, EDGE)]
    for r in range(ROWS):
        slab_ref[r] = feat_ref[:, r * EDGE:(r + 1) * EDGE]


def multiply_kernel(
    table_ref, tiles_ref, own_ref, arrived_ref, out_ref, list_ref, slab_ref, even_ref, odd_ref, sem
):
    to_smem = pltpu.make_async_copy(table_ref, list_ref, sem)
    to_smem.start()
    even_ref[...] = jnp.zeros(even_ref.shape, jnp.float32)
    odd_ref[...] = jnp.zeros(odd_ref.shape, jnp.float32)
    slab_ref[0] = jnp.zeros(slab_ref.shape[1:], slab_ref.dtype)
    slab_ref[1:ROWS + 1] = own_ref[...]
    slab_ref[ROWS + 1:] = arrived_ref[...]
    to_smem.wait()
    contract = (((1,), (1,)), ((), ()))

    def add_pair(part, at):
        item = list_ref[part * LIST_BLOCKS + (at >> 7), at & 127]
        both = item & 511
        row = (item >> 4) & 31
        tile = jnp.concatenate([tiles_ref[2 * both], tiles_ref[2 * both + 1]], axis=1)
        slab = jnp.concatenate([slab_ref[(item >> 9) & 255], slab_ref[item >> 17]], axis=1)
        if part == 0:
            even_ref[row] += lax.dot_general(tile, slab, contract, preferred_element_type=jnp.float32)
        else:
            odd_ref[row] += lax.dot_general(slab, tile, contract, preferred_element_type=jnp.float32)

    def chunk(i, carry):
        for u in range(0, EACH, 2):
            for part in range(2):
                for v in range(2):
                    add_pair(part, i * EACH + u + v)
        return carry

    longest = jnp.maximum(list_ref[LENGTH_ROW, 127], list_ref[LENGTH_ROW + 1, 127])
    lax.fori_loop(0, (longest + (EACH - 1)) // EACH, chunk, 0)
    owners = out_ref.shape[0]
    each = ROWS // owners
    for row in range(HALF):
        owner, j = divmod(2 * row, each)
        out_ref[owner, :, j * EDGE:(j + 1) * EDGE] = even_ref[row].astype(out_ref.dtype).T
        out_ref[owner, :, (j + 1) * EDGE:(j + 2) * EDGE] = odd_ref[row].astype(out_ref.dtype)


def per_device(features, tiles, tile_cols, tile_count, send_list, weight, bias):
    block_count, tile_depth, edge, _ = tiles.shape
    width = features.shape[1]
    feat_count = lax.axis_size("feat")
    vert_count = lax.axis_size("vert")
    bf16, f32, i32 = jnp.bfloat16, jnp.float32, jnp.int32
    whole = pl.BlockSpec(memory_space=VMEM)
    in_hbm = pl.BlockSpec(memory_space=pltpu.HBM)
    dma = pltpu.SemaphoreType.DMA
    mib = 1024 * 1024

    def stay(x):
        return pltpu.with_memory_space_constraint(x, pltpu.HBM)

    flat_tiles = pltpu.with_memory_space_constraint(
        tiles.reshape(block_count * tile_depth, edge, edge), VMEM
    )

    chosen, slabs, table = pl.pallas_call(
        pick_kernel,
        out_shape=(
            VMEM((block_count, width, edge), bf16),
            VMEM((block_count, width, edge), bf16),
            VMEM((LIST_ROWS, 128), i32),
        ),
        in_specs=[in_hbm] * 4,
        out_specs=(whole,) * 3,
        scratch_shapes=[
            SMEM(send_list.shape[:0:-1], i32),
            VMEM((width, block_count * edge), bf16),
            VMEM((tile_depth, block_count), i32),
            VMEM((1, block_count), i32),
            VMEM((32, block_count), f32),
            dma((4,)),
        ],
        name="pick",
        compiler_params=pltpu.CompilerParams(vmem_limit_bytes=4 * mib),
        cost_estimate=pl.CostEstimate(flops=20_000_000_000, bytes_accessed=200_000_000, transcendentals=0),
    )(
        stay(send_list[0].T), stay(features.T), stay(tile_cols.T),
        stay(tile_count.reshape(1, block_count)),
    )
    arrived = lax.all_to_all(
        chosen.reshape(vert_count, -1, width, edge), "vert", split_axis=0, concat_axis=0, tiled=True
    ).reshape(block_count, width, edge)

    hidden = pl.pallas_call(
        multiply_kernel,
        out_shape=jax.ShapeDtypeStruct((feat_count, width, block_count * edge // feat_count), bf16),
        in_specs=[whole, whole, whole, whole],
        out_specs=whole,
        scratch_shapes=[
            SMEM((LIST_ROWS, 128), i32),
            VMEM((SLOTS, width, edge), bf16),
            VMEM((HALF, edge, width), f32),
            VMEM((HALF, width, edge), f32),
            dma,
        ],
        name="multiply",
        compiler_params=pltpu.CompilerParams(vmem_limit_bytes=8 * mib),
        cost_estimate=pl.CostEstimate(
            flops=8_000_000_000, bytes_accessed=17_000_000, transcendentals=0
        ),
    )(table, flat_tiles, slabs, arrived)

    full_rows = lax.all_to_all(hidden, "feat", split_axis=0, concat_axis=0, tiled=True)
    full_rows = full_rows.reshape(feat_count * width, -1)
    mixed_rows = lax.dot_general(
        full_rows, weight, (((0,), (0,)), ((), ())), preferred_element_type=f32
    )
    return jnp.maximum(mixed_rows + bias, f32(0.0)).astype(bf16)


def solution(mesh):
    return jax.shard_map(
        per_device,
        mesh=mesh,
        in_specs=(
            P("vert", "feat"),
            P("vert", None, None, None),
            P("vert", None),
            P("vert"),
            P("vert", None, None),
            P(),
            P(),
        ),
        out_specs=P(("vert", "feat"), None),
        check_vma=False,
    )
```

profile of v0, /device:TPU:1, one launch (start us, length us, event | category | flops | bytes accessed | tf_op | source)
XLA Modules:
  0.0 41.8 jit_solution(8531861465839931704)
XLA Ops:
  0.0 0.0 copy-start
  0.0 0.0 copy-start.1
  0.0 1.5 %pick.1 = (bf16[64,16,128]{2,1,0:T(8,128)(2,1)S(1)}, bf16[64,16,128]{2,1,0:T(8,128)(2,1)S(1)}, s32[8,128]{1,0:T(8,128)S(1)}) custom-call(s32[4,16]{1,0:T(4,128)} %bitcast.18, bf16[16,8192]{1,0:T(8,128)(2,1)} %bitcast.16, s32[16,64]{1,0:T(8,128)} %bitcast.17, s32[1,64]{1,0:T(1,128)} %bitcast.19), custom_call_target="tpu_custom_call" | custom-call | flops 20000000000 | bytes 200000000 | tf_op jit(solution)/shard_map/pick/pallas_call | solution.py:162
  1.6 0.0 copy-start.2
  1.6 15.1 %all_to_all.10 = bf16[16,4,16,128]{3,2,1,0:T(8,128)(2,1)S(1)} all-to-all(bf16[16,4,16,128]{3,2,1,0:T(8,128)(2,1)S(1)} %bitcast.14), channel_id=1, replica_groups=mesh['vert'=16,'feat'=16] {'vert'}, dimensions={0} | all-to-all | bytes 524288 | tf_op jit(solution)/shard_map/all_to_all | solution.py:186
  16.7 0.0 copy-done.1
  16.7 2.2 %multiply.1 = bf16[16,16,512]{2,1,0:T(8,128)(2,1)S(1)} custom-call(s32[8,128]{1,0:T(8,128)S(1)} %get-tuple-element.8.table_ref, bf16[1024,128,128]{2,1,0:T(8,128)(2,1)S(1)} %bitcast.12, bf16[64,16,128]{2,1,0:T(8,128)(2,1)S(1)} %get-tuple-element.9.own_ref, bf16[64,16,128]{2,1,0:T(8,128)(2,1)S(1)} %bitcast.13), custom_call_target="tpu_custom_call" | custom-call | flops 8000000000 | bytes 17000000 | tf_op jit(solution)/shard_map/multiply/pallas_call | solution.py:190
  18.9 21.9 %all_to_all.11 = bf16[16,16,512]{2,1,0:T(8,128)(2,1)S(1)} all-to-all(bf16[16,16,512]{2,1,0:T(8,128)(2,1)S(1)} %multiply.1), channel_id=1, replica_groups=mesh['vert'=16,'feat'=16] {'feat'}, dimensions={0} | all-to-all | bytes 524288 | tf_op jit(solution)/shard_map/all_to_all | solution.py:209
  40.8 0.0 copy-done
  40.8 0.0 copy-done.2
  40.8 1.0 %fusion.1 = bf16[512,256]{1,0:T(8,128)(2,1)} fusion(bf16[256,512]{1,0:T(8,128)(2,1)S(1)} %bitcast.15, bf16[256,256]{1,0:T(8,128)(2,1)S(1)} %copy-done, f32[256]{0:T(256)S(1)} %copy-done.2), kind=kOutput, calls=%fused_computation.2 | convolution fusion | flops 67502080 | bytes 656384 | tf_op jit(solution)/shard_map/dot_general | solution.py:211
Async XLA Ops:
  0.0 40.8 %copy-start = (bf16[256,256]{1,0:T(8,128)(2,1)S(1)}, bf16[256,256]{1,0:T(8,128)(2,1)}, u32[]{:S(2)}) copy-start(bf16[256,256]{1,0:T(8,128)(2,1)} %param.12) | copy-start | bytes 393220
  0.0 16.7 %copy-start.1 = (bf16[64,16,128,128]{3,2,1,0:T(8,128)(2,1)S(1)}, bf16[64,16,128,128]{3,2,1,0:T(8,128)(2,1)}, u32[]{:S(2)}) copy-start(bf16[64,16,128,128]{3,2,1,0:T(8,128)(2,1)} %param.8) | copy-start | bytes 100663296
  1.6 39.2 %copy-start.2 = (f32[256]{0:T(256)S(1)}, f32[256]{0:T(256)}, u32[]{:S(2)}) copy-start(f32[256]{0:T(256)} %param.13) | copy-start | bytes 3076
where the time goes:
time: 42 us; the launch traced here: 41.8 us
  blocking collectives  37 us (88%)
  Pallas kernels  3.8 us (9%)
  matrix products  0.97 us (2%)
    all_to_all x1, blocking collectives, per_device(): lax.all_to_all(hidden, 'feat', split_axis=0, concat_axis=0, tiled=True)  21.9 us
    all_to_all x1, blocking collectives, per_device(): lax.all_to_all(chosen.reshape(vert_count, -1, width, edge), 'vert', split...  15.1 us
    pallas_call x1, Pallas kernels, per_device(): pl.pallas_call(multiply_kernel, out_shape=jax.ShapeDtypeStruct((feat_coun...  2.25 us
    pallas_call x1, Pallas kernels, per_device(): pl.pallas_call(pick_kernel, out_shape=(VMEM((block_count, width, edge), b...  1.55 us
    dot_general x1, matrix products, per_device(): lax.dot_general(full_rows, weight, (((0,), (0,)), ((), ())), preferred_el...  0.97 us

commit v1 on v0

--- a/solution.py
+++ b/solution.py
@@ -7,7 +7,7 @@
 
 VMEM = pltpu.VMEM
 SMEM = pltpu.SMEM
-EACH = 24
+EACH = 32
 PAIRS_MAX = 8
 ROWS = 64
 HALF = ROWS // 2
@@ -75,8 +75,8 @@
 
 
 def pick_kernel(
-    send_hbm, feat_hbm, cols_hbm, count_hbm, out_ref, slab_ref, table_ref,
-    send_ref, feat_ref, cols_ref, count_ref, piece_ref, sem,
+    send_hbm, feat_hbm, cols_hbm, count_hbm, out_ref, slab_ref, list_ref,
+    send_ref, feat_ref, cols_ref, count_ref, piece_ref, table_ref, sem,
 ):
     copies = [
         pltpu.make_async_copy(src, dst, sem.at[i])
@@ -89,6 +89,8 @@
     copies[1].wait()
     copies[2].wait()
     build_list(cols_ref, count_ref, piece_ref, table_ref)
+    to_smem = pltpu.make_async_copy(table_ref, list_ref, sem.at[4])
+    to_smem.start()
     copies[3].wait()
     copies[0].wait()
     slots, peers = send_ref.shape
@@ -98,19 +100,17 @@
             out_ref[peer * slots + slot] = feat_ref[:, pl.ds(start, EDGE)]
     for r in range(ROWS):
         slab_ref[r] = feat_ref[:, r * EDGE:(r + 1) * EDGE]
+    to_smem.wait()
 
 
 def multiply_kernel(
-    table_ref, tiles_ref, own_ref, arrived_ref, out_ref, list_ref, slab_ref, even_ref, odd_ref, sem
+    list_ref, tiles_ref, own_ref, arrived_ref, out_ref, slab_ref, even_ref, odd_ref
 ):
-    to_smem = pltpu.make_async_copy(table_ref, list_ref, sem)
-    to_smem.start()
     even_ref[...] = jnp.zeros(even_ref.shape, jnp.float32)
     odd_ref[...] = jnp.zeros(odd_ref.shape, jnp.float32)
     slab_ref[0] = jnp.zeros(slab_ref.shape[1:], slab_ref.dtype)
     slab_ref[1:ROWS + 1] = own_ref[...]
     slab_ref[ROWS + 1:] = arrived_ref[...]
-    to_smem.wait()
     contract = (((1,), (1,)), ((), ()))
 
     def add_pair(part, at):
@@ -148,6 +148,7 @@
     vert_count = lax.axis_size("vert")
     bf16, f32, i32 = jnp.bfloat16, jnp.float32, jnp.int32
     whole = pl.BlockSpec(memory_space=VMEM)
+    scalar = pl.BlockSpec(memory_space=SMEM)
     in_hbm = pl.BlockSpec(memory_space=pltpu.HBM)
     dma = pltpu.SemaphoreType.DMA
     mib = 1024 * 1024
@@ -164,17 +165,18 @@
         out_shape=(
             VMEM((block_count, width, edge), bf16),
             VMEM((block_count, width, edge), bf16),
-            VMEM((LIST_ROWS, 128), i32),
+            SMEM((LIST_ROWS, 128), i32),
         ),
         in_specs=[in_hbm] * 4,
-        out_specs=(whole,) * 3,
+        out_specs=(whole, whole, scalar),
         scratch_shapes=[
             SMEM(send_list.shape[:0:-1], i32),
             VMEM((width, block_count * edge), bf16),
             VMEM((tile_depth, block_count), i32),
             VMEM((1, block_count), i32),
             VMEM((32, block_count), f32),
-            dma((4,)),
+            VMEM((LIST_ROWS, 128), i32),
+            dma((5,)),
         ],
         name="pick",
         compiler_params=pltpu.CompilerParams(vmem_limit_bytes=4 * mib),
@@ -190,14 +192,12 @@
     hidden = pl.pallas_call(
         multiply_kernel,
         out_shape=jax.ShapeDtypeStruct((feat_count, width, block_count * edge // feat_count), bf16),
-        in_specs=[whole, whole, whole, whole],
+        in_specs=[scalar, whole, whole, whole],
         out_specs=whole,
         scratch_shapes=[
-            SMEM((LIST_ROWS, 128), i32),
             VMEM((SLOTS, width, edge), bf16),
             VMEM((HALF, edge, width), f32),
             VMEM((HALF, width, edge), f32),
-            dma,
         ],
         name="multiply",
         compiler_params=pltpu.CompilerParams(vmem_limit_bytes=8 * mib),

time: 42 us -> 41.9 us (level)
  Pallas kernels: 3.8 us -> 3.34 us
    pallas_call x1, Pallas kernels: 2.25 us -> 1.32 us  [per_device(): pl.pallas_call(multiply_kernel, out_shape=jax.ShapeDtypeStruct((feat_coun...]
    pallas_call x1, Pallas kernels: 1.55 us -> 2.02 us  [per_device(): pl.pallas_call(pick_kernel, out_shape=(VMEM((block_count, width, edge), b...]
where the time goes in v1:
time: 41.9 us; the launch traced here: 41.3 us
  blocking collectives  37 us (88%)
  Pallas kernels  3.34 us (8%)
  matrix products  0.98 us (2%)
    all_to_all x1, blocking collectives, per_device(): lax.all_to_all(hidden, 'feat', split_axis=0, concat_axis=0, tiled=True)  21.9 us
    all_to_all x1, blocking collectives, per_device(): lax.all_to_all(chosen.reshape(vert_count, -1, width, edge), 'vert', split...  15.1 us
    pallas_call x1, Pallas kernels, per_device(): pl.pallas_call(pick_kernel, out_shape=(VMEM((block_count, width, edge), b...  2.02 us
    pallas_call x1, Pallas kernels, per_device(): pl.pallas_call(multiply_kernel, out_shape=jax.ShapeDtypeStruct((feat_coun...  1.32 us
    dot_general x1, matrix products, per_device(): lax.dot_general(full_rows, weight, (((0,), (0,)), ((), ())), preferred_el...  0.98 us

profile of v1, /device:TPU:1, one launch (start us, length us, event | category | flops | bytes accessed | tf_op | source)
XLA Modules:
  0.0 41.3 jit_solution(3160060626308030876)
XLA Ops:
  0.0 0.0 copy-start
  0.0 0.0 copy-start.1
  0.0 2.0 %pick.1 = (bf16[64,16,128]{2,1,0:T(8,128)(2,1)S(1)}, bf16[64,16,128]{2,1,0:T(8,128)(2,1)S(1)}, s32[8,128]{1,0:T(8,128)S(4)}) custom-call(s32[4,16]{1,0:T(4,128)} %bitcast.18, bf16[16,8192]{1,0:T(8,128)(2,1)} %bitcast.16, s32[16,64]{1,0:T(8,128)} %bitcast.17, s32[1,64]{1,0:T(1,128)} %bitcast.19), custom_call_target="tpu_custom_call" | custom-call | flops 20000000000 | bytes 200000000 | tf_op jit(solution)/shard_map/pick/pallas_call | solution.py:163
  2.0 0.0 copy-start.2
  2.0 15.1 %all_to_all.10 = bf16[16,4,16,128]{3,2,1,0:T(8,128)(2,1)S(1)} all-to-all(bf16[16,4,16,128]{3,2,1,0:T(8,128)(2,1)S(1)} %bitcast.14), channel_id=1, replica_groups=mesh['vert'=16,'feat'=16] {'vert'}, dimensions={0} | all-to-all | bytes 524288 | tf_op jit(solution)/shard_map/all_to_all | solution.py:188
  17.1 0.0 copy-done.1
  17.1 1.3 %multiply.1 = bf16[16,16,512]{2,1,0:T(8,128)(2,1)S(1)} custom-call(s32[8,128]{1,0:T(8,128)S(4)} %get-tuple-element.8.list_ref, bf16[1024,128,128]{2,1,0:T(8,128)(2,1)S(1)} %bitcast.12, bf16[64,16,128]{2,1,0:T(8,128)(2,1)S(1)} %get-tuple-element.9.own_ref, bf16[64,16,128]{2,1,0:T(8,128)(2,1)S(1)} %bitcast.13), custom_call_target="tpu_custom_call" | custom-call | flops 8000000000 | bytes 17000000 | tf_op jit(solution)/shard_map/multiply/pallas_call | solution.py:192
  18.5 21.9 %all_to_all.11 = bf16[16,16,512]{2,1,0:T(8,128)(2,1)S(1)} all-to-all(bf16[16,16,512]{2,1,0:T(8,128)(2,1)S(1)} %multiply.1), channel_id=1, replica_groups=mesh['vert'=16,'feat'=16] {'feat'}, dimensions={0} | all-to-all | bytes 524288 | tf_op jit(solution)/shard_map/all_to_all | solution.py:209
  40.3 0.0 copy-done
  40.3 0.0 copy-done.2
  40.3 1.0 %fusion.1 = bf16[512,256]{1,0:T(8,128)(2,1)} fusion(bf16[256,512]{1,0:T(8,128)(2,1)S(1)} %bitcast.15, bf16[256,256]{1,0:T(8,128)(2,1)S(1)} %copy-done, f32[256]{0:T(256)S(1)} %copy-done.2), kind=kOutput, calls=%fused_computation.2 | convolution fusion | flops 67502080 | bytes 656384 | tf_op jit(solution)/shard_map/dot_general | solution.py:211
Async XLA Ops:
  0.0 40.3 %copy-start = (bf16[256,256]{1,0:T(8,128)(2,1)S(1)}, bf16[256,256]{1,0:T(8,128)(2,1)}, u32[]{:S(2)}) copy-start(bf16[256,256]{1,0:T(8,128)(2,1)} %param.12) | copy-start | bytes 393220
  0.0 17.1 %copy-start.1 = (bf16[64,16,128,128]{3,2,1,0:T(8,128)(2,1)S(1)}, bf16[64,16,128,128]{3,2,1,0:T(8,128)(2,1)}, u32[]{:S(2)}) copy-start(bf16[64,16,128,128]{3,2,1,0:T(8,128)(2,1)} %param.8) | copy-start | bytes 100663296
  2.0 38.3 %copy-start.2 = (f32[256]{0:T(256)S(1)}, f32[256]{0:T(256)}, u32[]{:S(2)}) copy-start(f32[256]{0:T(256)} %param.13) | copy-start | bytes 3076

commit v2 on v0

--- a/solution.py
+++ b/solution.py
@@ -14,7 +14,7 @@
 EDGE = 128
 SLOTS = 2 * ROWS + 1
 LIST_ROWS = 8
-LIST_BLOCKS = 3
+LIST_BLOCKS = 2
 LIST_SPAN = LIST_BLOCKS * 128
 LENGTH_ROW = 2 * LIST_BLOCKS
 
@@ -30,7 +30,7 @@
             piece_ref[8 * half + p:8 * half + p + 1, :] = slot.astype(f32)
     piece_ref[16:17, :] = lane_row.astype(f32)
     piece_ref[17:24, :] = jnp.zeros((7, ROWS), f32)
-    pairs_each = ((counts + 1) >> 1).astype(f32)
+    pairs_each = ((counts - 1) >> 1).astype(f32)
     odd = lane_row & 1
     for part in range(2):
         piece_ref[24 + part:25 + part, :] = jnp.where(odd == part, pairs_each, f32(0))
@@ -56,7 +56,7 @@
         chosen = lax.dot_general(pieces, inside, nn, preferred_element_type=f32)
         ahead = lax.dot_general(pairs, past, nn, preferred_element_type=f32)
         ahead = ahead[part:part + 1, :].astype(i32)
-        pair = spot_row - ahead
+        pair = spot_row - ahead + 1
         mine = p_row == pair
 
         def field(at):
@@ -75,17 +75,19 @@
 
 
 def pick_kernel(
-    send_hbm, feat_hbm, cols_hbm, count_hbm, out_ref, slab_ref, table_ref,
+    send_hbm, feat_hbm, cols_hbm, count_hbm, out_ref, slab_ref, table_ref, cols_out, count_out,
     send_ref, feat_ref, cols_ref, count_ref, piece_ref, sem,
 ):
     copies = [
         pltpu.make_async_copy(src, dst, sem.at[i])
-        for i, (src, dst) in enumerate(
-            [(feat_hbm, feat_ref), (cols_hbm, cols_ref), (count_hbm, count_ref), (send_hbm, send_ref)]
-        )
+        for i, (src, dst) in enumerate([
+            (feat_hbm, feat_ref), (cols_hbm, cols_ref), (count_hbm, count_ref), (send_hbm, send_ref),
+            (cols_hbm, cols_out), (count_hbm, count_out),
+        ])
     ]
     for copy in copies:
         copy.start()
+    slab_ref[0] = jnp.zeros(slab_ref.shape[1:], slab_ref.dtype)
     copies[1].wait()
     copies[2].wait()
     build_list(cols_ref, count_ref, piece_ref, table_ref)
@@ -97,38 +99,44 @@
             start = pl.multiple_of(send_ref[slot, peer] * EDGE, EDGE)
             out_ref[peer * slots + slot] = feat_ref[:, pl.ds(start, EDGE)]
     for r in range(ROWS):
-        slab_ref[r] = feat_ref[:, r * EDGE:(r + 1) * EDGE]
+        slab_ref[r + 1] = feat_ref[:, r * EDGE:(r + 1) * EDGE]
+    copies[4].wait()
+    copies[5].wait()
 
 
 def multiply_kernel(
-    table_ref, tiles_ref, own_ref, arrived_ref, out_ref, list_ref, slab_ref, even_ref, odd_ref, sem
+    cols_ref, count_ref, table_ref, tiles_ref, own_ref, arrived_ref, out_ref, slab_ref,
+    list_ref, even_ref, odd_ref, sem,
 ):
     to_smem = pltpu.make_async_copy(table_ref, list_ref, sem)
     to_smem.start()
-    even_ref[...] = jnp.zeros(even_ref.shape, jnp.float32)
-    odd_ref[...] = jnp.zeros(odd_ref.shape, jnp.float32)
-    slab_ref[0] = jnp.zeros(slab_ref.shape[1:], slab_ref.dtype)
-    slab_ref[1:ROWS + 1] = own_ref[...]
     slab_ref[ROWS + 1:] = arrived_ref[...]
+    contract = (((1,), (1,)), ((), ()))
+
+    def product(part, both, a, b):
+        tile = jnp.concatenate([tiles_ref[2 * both], tiles_ref[2 * both + 1]], axis=1)
+        slab = jnp.concatenate([slab_ref[a], slab_ref[b]], axis=1)
+        left, right = (tile, slab) if part == 0 else (slab, tile)
+        return lax.dot_general(left, right, contract, preferred_element_type=jnp.float32)
+
+    sums = (even_ref, odd_ref)
+    for first in range(0, ROWS, 4):
+        for part in range(2):
+            for row in (first + part, first + part + 2):
+                a = cols_ref[0, row] + 1
+                b = jnp.where(count_ref[0, row] > 1, cols_ref[1, row] + 1, 0)
+                sums[part][row // 2] = product(part, row * PAIRS_MAX, a, b)
     to_smem.wait()
-    contract = (((1,), (1,)), ((), ()))
-
-    def add_pair(part, at):
-        item = list_ref[part * LIST_BLOCKS + (at >> 7), at & 127]
-        both = item & 511
-        row = (item >> 4) & 31
-        tile = jnp.concatenate([tiles_ref[2 * both], tiles_ref[2 * both + 1]], axis=1)
-        slab = jnp.concatenate([slab_ref[(item >> 9) & 255], slab_ref[item >> 17]], axis=1)
-        if part == 0:
-            even_ref[row] += lax.dot_general(tile, slab, contract, preferred_element_type=jnp.float32)
-        else:
-            odd_ref[row] += lax.dot_general(slab, tile, contract, preferred_element_type=jnp.float32)
 
     def chunk(i, carry):
         for u in range(0, EACH, 2):
             for part in range(2):
                 for v in range(2):
-                    add_pair(part, i * EACH + u + v)
+                    at = i * EACH + u + v
+                    item = list_ref[part * LIST_BLOCKS + (at >> 7), at & 127]
+                    sums[part][(item >> 4) & 31] += product(
+                        part, item & 511, (item >> 9) & 255, item >> 17
+                    )
         return carry
 
     longest = jnp.maximum(list_ref[LENGTH_ROW, 127], list_ref[LENGTH_ROW + 1, 127])
@@ -148,6 +156,7 @@
     vert_count = lax.axis_size("vert")
     bf16, f32, i32 = jnp.bfloat16, jnp.float32, jnp.int32
     whole = pl.BlockSpec(memory_space=VMEM)
+    scalar = pl.BlockSpec(memory_space=SMEM)
     in_hbm = pl.BlockSpec(memory_space=pltpu.HBM)
     dma = pltpu.SemaphoreType.DMA
     mib = 1024 * 1024
@@ -159,22 +168,24 @@
         tiles.reshape(block_count * tile_depth, edge, edge), VMEM
     )
 
-    chosen, slabs, table = pl.pallas_call(
+    chosen, slabs, table, cols, counts = pl.pallas_call(
         pick_kernel,
         out_shape=(
             VMEM((block_count, width, edge), bf16),
-            VMEM((block_count, width, edge), bf16),
+            VMEM((SLOTS, width, edge), bf16),
             VMEM((LIST_ROWS, 128), i32),
+            SMEM((tile_depth, block_count), i32),
+            SMEM((1, block_count), i32),
         ),
         in_specs=[in_hbm] * 4,
-        out_specs=(whole,) * 3,
+        out_specs=(whole, whole, whole, scalar, scalar),
         scratch_shapes=[
             SMEM(send_list.shape[:0:-1], i32),
             VMEM((width, block_count * edge), bf16),
             VMEM((tile_depth, block_count), i32),
             VMEM((1, block_count), i32),
             VMEM((32, block_count), f32),
-            dma((4,)),
+            dma((6,)),
         ],
         name="pick",
         compiler_params=pltpu.CompilerParams(vmem_limit_bytes=4 * mib),
@@ -187,24 +198,27 @@
         chosen.reshape(vert_count, -1, width, edge), "vert", split_axis=0, concat_axis=0, tiled=True
     ).reshape(block_count, width, edge)
 
-    hidden = pl.pallas_call(
+    hidden, _ = pl.pallas_call(
         multiply_kernel,
-        out_shape=jax.ShapeDtypeStruct((feat_count, width, block_count * edge // feat_count), bf16),
-        in_specs=[whole, whole, whole, whole],
-        out_specs=whole,
+        out_shape=(
+            jax.ShapeDtypeStruct((feat_count, width, block_count * edge // feat_count), bf16),
+            VMEM((SLOTS, width, edge), bf16),
+        ),
+        in_specs=[scalar, scalar, whole, whole, whole, whole],
+        out_specs=(whole, whole),
         scratch_shapes=[
             SMEM((LIST_ROWS, 128), i32),
-            VMEM((SLOTS, width, edge), bf16),
             VMEM((HALF, edge, width), f32),
             VMEM((HALF, width, edge), f32),
             dma,
         ],
+        input_output_aliases={4: 1},
         name="multiply",
         compiler_params=pltpu.CompilerParams(vmem_limit_bytes=8 * mib),
         cost_estimate=pl.CostEstimate(
             flops=8_000_000_000, bytes_accessed=17_000_000, transcendentals=0
         ),
-    )(table, flat_tiles, slabs, arrived)
+    )(cols, counts, table, flat_tiles, slabs, arrived)
 
     full_rows = lax.all_to_all(hidden, "feat", split_axis=0, concat_axis=0, tiled=True)
     full_rows = full_rows.reshape(feat_count * width, -1)

time: 42 us -> 41.4 us (0.986)
  Pallas kernels: 3.8 us -> 3.1 us
    pallas_call x1, Pallas kernels: 2.25 us -> 1.54 us  [per_device(): pl.pallas_call(multiply_kernel, out_shape=(jax.ShapeDtypeStruct((feat_cou...]
where the time goes in v2:
time: 41.4 us; the launch traced here: 41.1 us
  blocking collectives  37 us (89%)
  Pallas kernels  3.1 us (7%)
  matrix products  0.98 us (2%)
    all_to_all x1, blocking collectives, per_device(): lax.all_to_all(hidden, 'feat', split_axis=0, concat_axis=0, tiled=True)  21.9 us
    all_to_all x1, blocking collectives, per_device(): lax.all_to_all(chosen.reshape(vert_count, -1, width, edge), 'vert', split...  15.1 us
    pallas_call x1, Pallas kernels, per_device(): pl.pallas_call(pick_kernel, out_shape=(VMEM((block_count, width, edge), b...  1.56 us
    pallas_call x1, Pallas kernels, per_device(): pl.pallas_call(multiply_kernel, out_shape=(jax.ShapeDtypeStruct((feat_cou...  1.54 us
    dot_general x1, matrix products, per_device(): lax.dot_general(full_rows, weight, (((0,), (0,)), ((), ())), preferred_el...  0.98 us

profile of v2, /device:TPU:1, one launch (start us, length us, event | category | flops | bytes accessed | tf_op | source)
XLA Modules:
  0.0 41.1 jit_solution(5259731185457675688)
XLA Ops:
  0.0 0.0 copy-start
  0.0 0.0 copy-start.1
  0.0 1.6 %pick.1 = (bf16[64,16,128]{2,1,0:T(8,128)(2,1)S(1)}, bf16[129,16,128]{2,1,0:T(8,128)(2,1)S(1)}, s32[8,128]{1,0:T(8,128)S(1)}, s32[16,64]{1,0:T(8,128)S(4)}, s32[1,64]{1,0:T(1,128)S(4)}) custom-call(s32[4,16]{1,0:T(4,128)} %bitcast.18, bf16[16,8192]{1,0:T(8,128)(2,1)} %bitcast.16, s32[16,64]{1,0:T(8,128)} %bitcast.17, s32[1,64]{1,0:T(1,128)} %bitcast.19), custom_call_target="tpu_custom_call" | custom-call | flops 20000000000 | bytes 200000000 | tf_op jit(solution)/shard_map/pick/pallas_call | solution.py:171
  1.6 0.0 copy-start.2
  1.6 15.1 %all_to_all.10 = bf16[16,4,16,128]{3,2,1,0:T(8,128)(2,1)S(1)} all-to-all(bf16[16,4,16,128]{3,2,1,0:T(8,128)(2,1)S(1)} %bitcast.14), channel_id=1, replica_groups=mesh['vert'=16,'feat'=16] {'vert'}, dimensions={0} | all-to-all | bytes 524288 | tf_op jit(solution)/shard_map/all_to_all | solution.py:197
  16.7 0.0 copy-done.1
  16.7 1.5 %multiply.1 = (bf16[16,16,512]{2,1,0:T(8,128)(2,1)S(1)}, bf16[129,16,128]{2,1,0:T(8,128)(2,1)S(1)}) custom-call(s32[16,64]{1,0:T(8,128)S(4)} %get-tuple-element.11.cols_ref, s32[1,64]{1,0:T(1,128)S(4)} %get-tuple-element.12.count_ref, s32[8,128]{1,0:T(8,128)S(1)} %get-tuple-element.13.table_ref, ...), custom_call_target="tpu_custom_call", output_to_operand_aliasing={{1}: (4, {})} | custom-call | flops 8000000000 | bytes 17000000 | tf_op jit(solution)/shard_map/multiply/pallas_call | solution.py:201
  18.2 21.9 %all_to_all.11 = bf16[16,16,512]{2,1,0:T(8,128)(2,1)S(1)} all-to-all(bf16[16,16,512]{2,1,0:T(8,128)(2,1)S(1)} %get-tuple-element.16), channel_id=1, replica_groups=mesh['vert'=16,'feat'=16] {'feat'}, dimensions={0} | all-to-all | bytes 524288 | tf_op jit(solution)/shard_map/all_to_all | solution.py:223
  40.1 0.0 copy-done
  40.1 0.0 copy-done.2
  40.1 1.0 %fusion.1 = bf16[512,256]{1,0:T(8,128)(2,1)} fusion(bf16[256,512]{1,0:T(8,128)(2,1)S(1)} %bitcast.15, bf16[256,256]{1,0:T(8,128)(2,1)S(1)} %copy-done, f32[256]{0:T(256)S(1)} %copy-done.2), kind=kOutput, calls=%fused_computation.2 | convolution fusion | flops 67502080 | bytes 656384 | tf_op jit(solution)/shard_map/dot_general | solution.py:225
Async XLA Ops:
  0.0 40.1 %copy-start = (bf16[256,256]{1,0:T(8,128)(2,1)S(1)}, bf16[256,256]{1,0:T(8,128)(2,1)}, u32[]{:S(2)}) copy-start(bf16[256,256]{1,0:T(8,128)(2,1)} %param.12) | copy-start | bytes 393220
  0.0 16.7 %copy-start.1 = (bf16[64,16,128,128]{3,2,1,0:T(8,128)(2,1)S(1)}, bf16[64,16,128,128]{3,2,1,0:T(8,128)(2,1)}, u32[]{:S(2)}) copy-start(bf16[64,16,128,128]{3,2,1,0:T(8,128)(2,1)} %param.8) | copy-start | bytes 100663296
  1.6 38.5 %copy-start.2 = (f32[256]{0:T(256)S(1)}, f32[256]{0:T(256)}, u32[]{:S(2)}) copy-start(f32[256]{0:T(256)} %param.13) | copy-start | bytes 3076
